TPU v7x, 768 devices: a whole 4x8x12 slice. The times are simulated.
768 devices in a mesh: space: 24 (over x, z_lo), batch: 32 (over z_hi, y, core).
Axes of the slice: x: 4, y: 8, z: 12 (z_hi: 2, z_lo: 6; z = z_hi * 6 + z_lo), core: 2. Of those that a mesh axis runs over, the one named last changes fastest.
Arguments:
- pre_act: bfloat16 [32, 64, 24, 8, 128], P('batch', None, 'space'), may hold values from -6 to 6
- grad_out: bfloat16 [32, 128, 24, 8, 128], P('batch', None, 'space'), may hold values from -6 to 6
- weight: bfloat16 [27, 64, 128], replicated, may hold values from -0.109375 to 0.109375
Outputs:
- grad_in: bfloat16 [32, 64, 24, 8, 128], P('batch', None, 'space')
- weight_grad: float32 [221184], P(('space', 'batch'))
All inputs are finite; a program needn't handle non-finite values.
Results may differ from a plain program's by a relative error of at most 0.001.
Values may be sent and summed in bfloat16 or wider, within the bound.
No kernel may reach another device: no remote copies, remote signals or barrier semaphores. Data moves between devices by JAX's collectives and lax.ppermute only.
A program may use at most 32 MiB of HBM per device.

v0:
```python
import functools

import jax
import jax.numpy as jnp
from jax import lax
from jax.experimental import pallas as pl
from jax.experimental.pallas import tpu as pltpu
from jax.sharding import PartitionSpec as P


slope = 0.3
CIN, COUT, YC, ZC, TAPS = 64, 128, 8, 128, 27
CELLS = YC * ZC
ROWS = TAPS * CIN
XS, ZL, ZH, YS, CS = 4, 6, 2, 8, 2
ZS, YCS = ZL * ZH, YS * CS
XROWS = ROWS // XS
ZROWS = XROWS // ZS
PART = 3
XMARKS, YMARKS = 8, 4
TOP = 12.0


def shifted_lanes(tile, by):
    lane = lax.broadcasted_iota(jnp.int32, tile.shape, 1)
    if by > 0:
        return jnp.where(lane > 0, pltpu.roll(tile, 1, 1), 0.0)
    return jnp.where(lane < ZC - 1, pltpu.roll(tile, ZC - 1, 1), 0.0)


def spread(ref, wide, grads, first):
    wide[...] = ref[...].astype(jnp.float32).reshape(COUT * YC, ZC)
    for y in range(YC):
        tile = wide[pl.ds(y, COUT, stride=YC), :]
        for w in (-1, 0, 1):
            moved = tile if w == 0 else shifted_lanes(tile, w)
            row = first + (w + 1) * COUT
            grads[row : row + COUT, y * ZC : (y + 1) * ZC] = moved.astype(jnp.bfloat16)


def by_taps(hids, grads):
    return lax.dot_general(
        hids[...], grads[...], (((1,), (1,)), ((), ())), preferred_element_type=jnp.float32
    )


def by_cells(weights, grads):
    return lax.dot_general(
        weights[...], grads[...], (((1,), (0,)), ((), ())), preferred_element_type=jnp.float32
    )


def stack_hidden(act, acts, hids):
    hidden = jnp.where(act > 0, act, slope * act).astype(jnp.bfloat16)
    acts[...] = hidden.astype(jnp.float32).reshape(CIN * YC, ZC)
    for y in range(YC):
        tile = acts[pl.ds(y, CIN, stride=YC), :].astype(jnp.bfloat16)
        for v in (-1, 0, 1):
            if 0 <= y - v < YC:
                hids[(v + 1) * CIN : (v + 2) * CIN, (y - v) * ZC : (y - v + 1) * ZC] = tile
    none = jnp.zeros((CIN, ZC), jnp.bfloat16)
    hids[0:CIN, 0:ZC] = none
    hids[2 * CIN : 3 * CIN, (YC - 1) * ZC : YC * ZC] = none


def own_kernel(
    act_hbm, own_hbm, w_hbm, grad_ref, tap_ref, sum_ref, up_ref, down_ref, act_ref, own_ref, w_ref, wide, acts, hids, mids, sems
):
    pairs = ((own_hbm, own_ref), (act_hbm, act_ref), (w_hbm, w_ref))
    copies = [pltpu.make_async_copy(a, b, sems.at[i]) for i, (a, b) in enumerate(pairs)]
    for copy in copies:
        copy.start()
    copies[0].wait()
    spread(own_ref, wide, grad_ref, 0)
    copies[1].wait()
    stack_hidden(act_ref[...].astype(jnp.float32), acts, hids)
    copies[2].wait()
    for v in range(3):
        for w in range(3):
            rows, lanes = slice(v * CIN, (v + 1) * CIN), slice(w * COUT, (w + 1) * COUT)
            down_ref[rows, lanes] = w_ref[3 * v + w]
            mids[rows, lanes] = w_ref[9 + 3 * v + w]
            up_ref[rows, lanes] = w_ref[18 + 3 * v + w]
    tap_ref[...] = by_taps(hids, grad_ref)
    sum_ref[...] = by_cells(mids, grad_ref)


def chosen(take, swapped, straight):
    return jnp.where(take, swapped[...].astype(jnp.float32), straight[...].astype(jnp.float32))


def side_kernel(
    factor, at_ref, low_ref, high_ref, swap_ref, grad_ref, tap_ref, sent_ref, acts, hids
):
    at = at_ref[0, 0]
    stack_hidden(chosen(at == 0, swap_ref, low_ref), acts, hids)
    below = by_taps(hids, grad_ref)
    stack_hidden(chosen(at == ZL - 1, swap_ref, high_ref), acts, hids)
    above = by_taps(hids, grad_ref)
    taps = (below, tap_ref[...], above)
    most = functools.reduce(jnp.maximum, [jnp.max(jnp.abs(t), keepdims=True) for t in taps])
    exponent = jnp.floor(jnp.log2(jnp.maximum(most * factor, 1e-30))) + 1.0
    scale = jnp.broadcast_to(jnp.exp2(TOP - exponent) * factor, (CIN, COUT))
    for x in range(XS):
        sent_ref[x, XROWS : XROWS + XMARKS, :] = jnp.broadcast_to(exponent, (XMARKS, COUT))
    for tap in range(TAPS):
        u, v, w = tap // 9, tap // 3 % 3, tap % 3
        block = taps[u][v * CIN : (v + 1) * CIN, w * COUT : (w + 1) * COUT] * scale
        first = tap * CIN
        while first < (tap + 1) * CIN:
            x = first // XROWS
            last = min((tap + 1) * CIN, (x + 1) * XROWS)
            sent_ref[x, first - x * XROWS : last - x * XROWS, :] = block[first - tap * CIN : last - tap * CIN]
            first = last


def grad_kernel(
    at_ref, act_ref, low_ref, high_ref, swap_ref, sum_ref, up_ref, down_ref, gin_ref, plane, wide, acts, grads
):
    at = at_ref[0, 0]
    plane[...] = chosen(at == 0, swap_ref, low_ref)
    spread(plane, wide, grads, 0)
    sums = by_cells(up_ref, grads) + sum_ref[...]
    plane[...] = chosen(at == ZL - 1, swap_ref, high_ref)
    spread(plane, wide, grads, 0)
    sums = sums + by_cells(down_ref, grads)
    for y in range(YC):
        total = sums[CIN : 2 * CIN, y * ZC : (y + 1) * ZC]
        if y + 1 < YC:
            total = total + sums[0:CIN, (y + 1) * ZC : (y + 2) * ZC]
        if y - 1 >= 0:
            total = total + sums[2 * CIN : 3 * CIN, (y - 1) * ZC : y * ZC]
        acts[pl.ds(y, CIN, stride=YC), :] = total
    grad_hidden = acts[...].reshape(CIN, YC, ZC)
    act = act_ref[...].astype(jnp.float32)
    gin_ref[...] = (grad_hidden * jnp.where(act > 0, 1.0, slope)).astype(jnp.bfloat16)


def after_x_kernel(got_ref, sent_ref, total):
    exps = [got_ref[i, XROWS : XROWS + 1, :] for i in range(XS)]
    largest = functools.reduce(jnp.maximum, exps) + 2.0
    total[...] = sum(got_ref[i, 0:XROWS, :] * jnp.exp2(exps[i] - largest) for i in range(XS))
    for part in range(YCS):
        row = 9 * (part // 4) + 2 * (part % 4)
        for i in range(PART):
            sent_ref[part, i * ZS : (i + 1) * ZS, :] = total[pl.ds(row + i, ZS, stride=ZROWS), :]
        sent_ref[part, PART * ZS : PART * ZS + YMARKS, :] = jnp.broadcast_to(largest, (YMARKS, COUT))


def after_y_kernel(got_ref, sent_ref):
    total = jnp.zeros((PART * ZS, COUT), jnp.float32)
    for i in range(YCS):
        weight = jnp.exp2(got_ref[i, PART * ZS : PART * ZS + 1, :] - TOP)
        total = total + got_ref[i, 0 : PART * ZS, :] * weight
    for i in range(PART):
        sent_ref[:, i, :] = total[i * ZS : (i + 1) * ZS]


def call(body, outs, scratch, flops, *args, inputs=pltpu.VMEM):
    vmem = pl.BlockSpec(memory_space=pltpu.VMEM)
    given = pl.BlockSpec(memory_space=inputs)
    smem = pl.BlockSpec(memory_space=pltpu.SMEM)
    return pl.pallas_call(
        body,
        out_shape=tuple(jax.ShapeDtypeStruct(shape, dtype) for shape, dtype in outs),
        in_specs=[smem if arg.dtype == jnp.int32 else given for arg in args],
        out_specs=tuple([vmem] * len(outs)),
        scratch_shapes=[pltpu.VMEM(*x) if isinstance(x, tuple) else x for x in scratch],
        compiler_params=pltpu.CompilerParams(vmem_limit_bytes=16 * 1024 * 1024),
        cost_estimate=pl.CostEstimate(flops=flops, bytes_accessed=2_000_000, transcendentals=0),
    )(*args)


def device(x, zl, zh, y, c):
    return (x * ZL + zl) * ZH * YCS + zh * YCS + y * CS + c


def groups():
    along_x = [[x * ZL + zl for x in range(XS)] for zl in range(ZL)]
    along_y = [[zh * YCS + i for i in range(YCS)] for zh in range(ZH)]
    along_z = [
        [device(x, zl, zh, y, c) for zl in range(ZL) for zh in range(ZH)]
        for x in range(XS)
        for y in range(YS)
        for c in range(CS)
    ]
    return along_x, along_y, along_z


def exchanged(x, axis, members):
    return lax.all_to_all(x, axis, 0, 0, tiled=True, axis_index_groups=members)


def sent_along(value, pairs):
    return lax.ppermute(value, "space", pairs)


def gradients(pre_act, grad_out, weight):
    f32, bf16, f16 = jnp.float32, jnp.bfloat16, jnp.float16
    count = pre_act.shape[0] * lax.axis_size("batch") * lax.axis_size("space") * CELLS
    factor = float(1.0 / count**0.5)
    steps = XS * ZL
    forward = [(i, i + 1) for i in range(steps - 1) if (i + 1) % ZL]
    backward = [(target, source) for source, target in forward]
    turns = [(i, i + 1) for i in range(steps - 1) if (i + 1) % ZL == 0]
    turns = turns + [(target, source) for source, target in turns]
    along_x, along_y, along_z = groups()

    act = pre_act.reshape(CIN, YC, ZC)
    own = grad_out.reshape(COUT, YC, ZC)
    swap_act = sent_along(act, turns)
    low_act = sent_along(act, forward)
    high_act = sent_along(act, backward)
    low = sent_along(own, forward)
    plane = ((COUT * YC, ZC), f32)
    small = ((CIN * YC, ZC), f32)
    stacked, moved, third = ((3 * CIN, CELLS), bf16), ((3 * COUT, CELLS), bf16), ((3 * CIN, 3 * COUT), bf16)
    grads, taps, sums, up, down = call(
        own_kernel,
        [moved, ((3 * CIN, 3 * COUT), f32), ((3 * CIN, CELLS), f32), third, third],
        [(act.shape, bf16), (own.shape, bf16), (weight.shape, bf16), plane, small, stacked, third]
        + [pltpu.SemaphoreType.DMA((3,))],
        1_000_000_000,
        *[pltpu.with_memory_space_constraint(x, pltpu.HBM) for x in (act, own, weight)],
        inputs=pltpu.HBM,
    )
    start = (lax.axis_index("batch") & 3) * 32
    at = (lax.axis_index("space") % ZL).astype(jnp.int32).reshape(1, 1)
    start, at, taps = lax.optimization_barrier((start, at, taps))
    (sent,) = call(
        functools.partial(side_kernel, factor),
        [((XS, XROWS + XMARKS, COUT), f32)],
        [small, stacked],
        1_000_000_000,
        at, low_act, high_act, swap_act, grads, taps,
    )
    got = exchanged(sent.astype(f16), "space", along_x).astype(f32)
    (sent,) = call(after_x_kernel, [((YCS, PART * ZS + YMARKS, COUT), f32)], [((XROWS, COUT), f32)], 1_000_000, got)
    own, sent = lax.optimization_barrier((own, sent))
    high = sent_along(own, backward)
    swap_grad = sent_along(own, turns)
    got = exchanged(sent.astype(f16), "batch", along_y).astype(f32)
    (sent,) = call(after_y_kernel, [((ZS, PART, COUT), f32)], [], 1_000_000, got)
    sums, _ = lax.optimization_barrier((sums, sent))
    (grad_in,) = call(
        grad_kernel,
        [((CIN, YC, ZC), bf16)],
        [((COUT, YC, ZC), f32), plane, small, moved],
        2_000_000_000,
        at, act, low, high, swap_grad, sums, up, down,
    )
    got = exchanged(sent, ("space", "batch"), along_z)
    total = jnp.sum(got, axis=0).reshape(-1)
    weight_grad = lax.dynamic_slice(total, (start,), (ROWS * COUT // 768,))
    return (grad_in.reshape(pre_act.shape), weight_grad)


def solution(mesh):
    return jax.shard_map(
        gradients,
        mesh=mesh,
        in_specs=(
            P("batch", None, "space", None, None),
            P("batch", None, "space", None, None),
            P(),
        ),
        out_specs=(P("batch", None, "space", None, None), P(("space", "batch"))),
        check_vma=False,
    )
```

profile of v0, /device:TPU:10, one launch (start us, length us, event | category | flops | bytes accessed | tf_op | source)
XLA Modules:
  0.0 80.3 jit_solution(16651688469199584702)
XLA Ops:
  0.6 4.3 %collective-permute-start.1 = (bf16[64,8,128]{2,1,0:T(8,128)(2,1)}, bf16[64,8,128]{2,1,0:T(8,128)(2,1)S(1)}, u32[]{:S(2)}, u32[]{:S(2)}) collective-permute-start(bf16[64,8,128]{2,1,0:T(8,128)(2,1)} %bitcast.7), channel_id=1, source_target_pairs={{0,32},{32,64},{64,96},{96,128},{128,160},{192,224},{224,256},{256... | collective-permute-start | bytes 393224 | tf_op jit(solution)/shard_map/ppermute | solution.py:195
  4.9 1.3 %collective-permute-start.2 = (bf16[64,8,128]{2,1,0:T(8,128)(2,1)}, bf16[64,8,128]{2,1,0:T(8,128)(2,1)S(1)}, u32[]{:S(2)}, u32[]{:S(2)}) collective-permute-start(bf16[64,8,128]{2,1,0:T(8,128)(2,1)} %bitcast.8), channel_id=1, source_target_pairs={{32,0},{64,32},{96,64},{128,96},{160,128},{224,192},{256,224},{288... | collective-permute-start | bytes 393224 | tf_op jit(solution)/shard_map/ppermute | solution.py:195
  6.2 13.0 %collective-permute-start.3 = (bf16[64,8,128]{2,1,0:T(8,128)(2,1)}, bf16[64,8,128]{2,1,0:T(8,128)(2,1)S(1)}, u32[]{:S(2)}, u32[]{:S(2)}) collective-permute-start(bf16[64,8,128]{2,1,0:T(8,128)(2,1)} %bitcast.9), channel_id=1, source_target_pairs={{160,192},{352,384},{544,576},{192,160},{384,352},{576,544},{161,1... | collective-permute-start | bytes 393224 | tf_op jit(solution)/shard_map/ppermute | solution.py:195
  19.2 2.1 %shard_map.50 = (bf16[384,1024]{1,0:T(8,128)(2,1)S(1)}, f32[192,384]{1,0:T(8,128)S(1)}, f32[192,1024]{1,0:T(8,128)S(1)}, bf16[192,384]{1,0:T(8,128)(2,1)S(1)}, bf16[192,384]{1,0:T(8,128)(2,1)S(1)}) custom-call(bf16[64,8,128]{2,1,0:T(8,128)(2,1)} %bitcast.10, bf16[128,8,128]{2,1,0:T(8,128)(2,1)} %bitcast.13, bf16[27,64,128]{2,1,0:T(8,128)(2,1)} %w_hbm.1), custom_call_target="tpu_custom_call" | custom-call | flops 1000000000 | bytes 2000000 | tf_op jit(solution)/shard_map/pallas_call | solution.py:163
  21.3 0.0 collective-permute-done.1.low_ref
  21.3 0.0 collective-permute-done.2.high_ref
  21.3 1.9 %collective-permute-done.3.swap_ref = bf16[64,8,128]{2,1,0:T(8,128)(2,1)S(1)} collective-permute-done((bf16[64,8,128]{2,1,0:T(8,128)(2,1)}, bf16[64,8,128]{2,1,0:T(8,128)(2,1)S(1)}, u32[]{:S(2)}, u32[]{:S(2)}) %collective-permute-start.3) | collective-permute-done | bytes 131104 | tf_op jit(solution)/shard_map/ppermute | solution.py:195
  23.2 1.1 %shard_map.51 = f32[4,440,128]{2,1,0:T(8,128)S(1)} custom-call(s32[1,1]{1,0:T(1,128)} %bitcast.at_ref, bf16[64,8,128]{2,1,0:T(8,128)(2,1)S(1)} %collective-permute-done.1.low_ref, bf16[64,8,128]{2,1,0:T(8,128)(2,1)S(1)} %collective-permute-done.2.high_ref, bf16[64,8,128]{2,1,0:T(8,128)(2,1)S(1)} %collective-permute-done.3.swap_ref, ...), custom_call_target="tpu_custom_call" | custom-call | flops 1000000000 | bytes 2000000 | tf_op jit(solution)/shard_map/pallas_call | solution.py:163
  24.3 0.1 convert_element_type.12
  24.4 11.3 %all_to_all.15 = f16[4,440,128]{2,1,0:T(8,128)(2,1)S(1)} all-to-all(f16[4,440,128]{2,1,0:T(8,128)(2,1)S(1)} %convert_element_type.12), channel_id=1, replica_groups={{0,192,384,576},{32,224,416,608},{64,256,448,640},{96,288,480,672},{128..., dimensions={0} | all-to-all | bytes 901120 | tf_op jit(solution)/shard_map/all_to_all | solution.py:191
  35.6 0.1 convert_element_type.13.got_ref
  35.7 0.1 shard_map.52
  35.8 0.7 convert_element_type.14
  36.5 0.0 copy-start.1
  36.5 7.7 %all-to-all-start.1 = ((f16[16,40,128]{2,1,0:T(8,128)(2,1)}), f16[16,40,128]{2,1,0:T(8,128)(2,1)S(1)}, u32[]{:S(2)}, u32[]{:S(2)}) async-start(f16[16,40,128]{2,1,0:T(8,128)(2,1)} %convert_element_type.14), calls=%async_computation.1 | async-start | bytes 327680 | tf_op jit(solution)/shard_map/all_to_all | solution.py:191
  44.2 0.0 copy-done.1
  44.2 1.3 %collective-permute-start = (bf16[128,8,128]{2,1,0:T(8,128)(2,1)S(1)}, bf16[128,8,128]{2,1,0:T(8,128)(2,1)S(1)}, u32[]{:S(2)}, u32[]{:S(2)}) collective-permute-start(bf16[128,8,128]{2,1,0:T(8,128)(2,1)S(1)} %bitcast.14), channel_id=1, source_target_pairs={{0,32},{32,64},{64,96},{96,128},{128,160},{192,224},{224,256},{256... | collective-permute-start | bytes 786440 | tf_op jit(solution)/shard_map/ppermute | solution.py:195
  45.5 1.3 %collective-permute-start.4 = (bf16[128,8,128]{2,1,0:T(8,128)(2,1)S(1)}, bf16[128,8,128]{2,1,0:T(8,128)(2,1)S(1)}, u32[]{:S(2)}, u32[]{:S(2)}) collective-permute-start(bf16[128,8,128]{2,1,0:T(8,128)(2,1)S(1)} %bitcast.15), channel_id=1, source_target_pairs={{32,0},{64,32},{96,64},{128,96},{160,128},{224,192},{256,224},{288... | collective-permute-start | bytes 786440 | tf_op jit(solution)/shard_map/ppermute | solution.py:195
  46.8 12.5 %collective-permute-start.5 = (bf16[128,8,128]{2,1,0:T(8,128)(2,1)S(1)}, bf16[128,8,128]{2,1,0:T(8,128)(2,1)S(1)}, u32[]{:S(2)}, u32[]{:S(2)}) collective-permute-start(bf16[128,8,128]{2,1,0:T(8,128)(2,1)S(1)} %bitcast.16), channel_id=1, source_target_pairs={{160,192},{352,384},{544,576},{192,160},{384,352},{576,544},{161,1... | collective-permute-start | bytes 786440 | tf_op jit(solution)/shard_map/ppermute | solution.py:195
  59.4 0.0 all-to-all-done.1
  59.4 0.0 copy-start
  59.4 0.7 shard_map.53
  60.1 9.4 %all-to-all-start.2 = ((f32[12,3,128]{2,1,0:T(4,128)}), f32[12,3,128]{2,1,0:T(4,128)S(1)}, u32[]{:S(2)}, u32[]{:S(2)}) async-start(f32[12,3,128]{2,1,0:T(4,128)} %shard_map.53), calls=%async_computation.2 | async-start | bytes 49152 | tf_op jit(solution)/shard_map/all_to_all | solution.py:191
  69.5 0.0 collective-permute-done.low_ref
  69.5 0.0 collective-permute-done.4.high_ref
  69.5 0.0 collective-permute-done.5.swap_ref
  69.6 0.0 copy-done
  69.6 1.6 %shard_map.54 = bf16[64,8,128]{2,1,0:T(8,128)(2,1)} custom-call(s32[1,1]{1,0:T(1,128)} %bitcast.at_ref, bf16[64,8,128]{2,1,0:T(8,128)(2,1)S(1)} %bitcast.11, bf16[128,8,128]{2,1,0:T(8,128)(2,1)S(1)} %collective-permute-done.low_ref, bf16[128,8,128]{2,1,0:T(8,128)(2,1)S(1)} %collective-permute-done.4.high_ref, ...), custom_call_target="tpu_custom_call" | custom-call | flops 2000000000 | bytes 2000000 | tf_op jit(solution)/shard_map/pallas_call | solution.py:163
  71.2 8.5 %all-to-all-done.2 = f32[12,3,128]{2,1,0:T(4,128)S(1)} async-done(((f32[12,3,128]{2,1,0:T(4,128)}), f32[12,3,128]{2,1,0:T(4,128)S(1)}, u32[]{:S(2)}, u32[]{:S(2)}) %all-to-all-start.2) | async-done | bytes 18464 | tf_op jit(solution)/shard_map/all_to_all | solution.py:191
  79.7 0.7 dynamic_slice.3
  (2 shorter events, 0.0 us)
Async XLA Ops:
  0.6 20.7 %collective-permute-start.1 = (bf16[64,8,128]{2,1,0:T(8,128)(2,1)}, bf16[64,8,128]{2,1,0:T(8,128)(2,1)S(1)}, u32[]{:S(2)}, u32[]{:S(2)}) collective-permute-start(bf16[64,8,128]{2,1,0:T(8,128)(2,1)} %bitcast.7), channel_id=1, source_target_pairs={{0,32},{32,64},{64,96},{96,128},{128,160},{192,224},{224,256},{256... | collective-permute-start | bytes 393224 | tf_op jit(solution)/shard_map/ppermute | solution.py:195
  4.9 16.4 %collective-permute-start.2 = (bf16[64,8,128]{2,1,0:T(8,128)(2,1)}, bf16[64,8,128]{2,1,0:T(8,128)(2,1)S(1)}, u32[]{:S(2)}, u32[]{:S(2)}) collective-permute-start(bf16[64,8,128]{2,1,0:T(8,128)(2,1)} %bitcast.8), channel_id=1, source_target_pairs={{32,0},{64,32},{96,64},{128,96},{160,128},{224,192},{256,224},{288... | collective-permute-start | bytes 393224 | tf_op jit(solution)/shard_map/ppermute | solution.py:195
  6.2 17.0 %collective-permute-start.3 = (bf16[64,8,128]{2,1,0:T(8,128)(2,1)}, bf16[64,8,128]{2,1,0:T(8,128)(2,1)S(1)}, u32[]{:S(2)}, u32[]{:S(2)}) collective-permute-start(bf16[64,8,128]{2,1,0:T(8,128)(2,1)} %bitcast.9), channel_id=1, source_target_pairs={{160,192},{352,384},{544,576},{192,160},{384,352},{576,544},{161,1... | collective-permute-start | bytes 393224 | tf_op jit(solution)/shard_map/ppermute | solution.py:195
  36.5 7.7 %copy-start.1 = (bf16[1,128,1,8,128]{4,3,2,1,0:T(8,128)(2,1)S(1)}, bf16[1,128,1,8,128]{4,3,2,1,0:T(8,128)(2,1)}, u32[]{:S(2)}) copy-start(bf16[1,128,1,8,128]{4,3,2,1,0:T(8,128)(2,1)} %param.4) | copy-start | bytes 786436
  36.5 22.8 %all-to-all-start.1 = ((f16[16,40,128]{2,1,0:T(8,128)(2,1)}), f16[16,40,128]{2,1,0:T(8,128)(2,1)S(1)}, u32[]{:S(2)}, u32[]{:S(2)}) async-start(f16[16,40,128]{2,1,0:T(8,128)(2,1)} %convert_element_type.14), calls=%async_computation.1 | async-start | bytes 327680 | tf_op jit(solution)/shard_map/all_to_all | solution.py:191
  44.2 25.3 %collective-permute-start = (bf16[128,8,128]{2,1,0:T(8,128)(2,1)S(1)}, bf16[128,8,128]{2,1,0:T(8,128)(2,1)S(1)}, u32[]{:S(2)}, u32[]{:S(2)}) collective-permute-start(bf16[128,8,128]{2,1,0:T(8,128)(2,1)S(1)} %bitcast.14), channel_id=1, source_target_pairs={{0,32},{32,64},{64,96},{96,128},{128,160},{192,224},{224,256},{256... | collective-permute-start | bytes 786440 | tf_op jit(solution)/shard_map/ppermute | solution.py:195
  45.5 24.0 %collective-permute-start.4 = (bf16[128,8,128]{2,1,0:T(8,128)(2,1)S(1)}, bf16[128,8,128]{2,1,0:T(8,128)(2,1)S(1)}, u32[]{:S(2)}, u32[]{:S(2)}) collective-permute-start(bf16[128,8,128]{2,1,0:T(8,128)(2,1)S(1)} %bitcast.15), channel_id=1, source_target_pairs={{32,0},{64,32},{96,64},{128,96},{160,128},{224,192},{256,224},{288... | collective-permute-start | bytes 786440 | tf_op jit(solution)/shard_map/ppermute | solution.py:195
  46.8 22.7 %collective-permute-start.5 = (bf16[128,8,128]{2,1,0:T(8,128)(2,1)S(1)}, bf16[128,8,128]{2,1,0:T(8,128)(2,1)S(1)}, u32[]{:S(2)}, u32[]{:S(2)}) collective-permute-start(bf16[128,8,128]{2,1,0:T(8,128)(2,1)S(1)} %bitcast.16), channel_id=1, source_target_pairs={{160,192},{352,384},{544,576},{192,160},{384,352},{576,544},{161,1... | collective-permute-start | bytes 786440 | tf_op jit(solution)/shard_map/ppermute | solution.py:195
  59.4 10.2 %copy-start = (bf16[1,64,1,8,128]{4,3,2,1,0:T(8,128)(2,1)S(1)}, bf16[1,64,1,8,128]{4,3,2,1,0:T(8,128)(2,1)}, u32[]{:S(2)}) copy-start(bf16[1,64,1,8,128]{4,3,2,1,0:T(8,128)(2,1)} %param.3) | copy-start | bytes 393220
  60.1 19.6 %all-to-all-start.2 = ((f32[12,3,128]{2,1,0:T(4,128)}), f32[12,3,128]{2,1,0:T(4,128)S(1)}, u32[]{:S(2)}, u32[]{:S(2)}) async-start(f32[12,3,128]{2,1,0:T(4,128)} %shard_map.53), calls=%async_computation.2 | async-start | bytes 49152 | tf_op jit(solution)/shard_map/all_to_all | solution.py:191
where the time goes:
time: 80.7 us; the launch traced here: 80.3 us
  starting transfers between devices  50.8 us (63%)
  blocking collectives  11.3 us (14%)
  waiting for transfers between devices  10.4 us (13%)
  Pallas kernels  5.54 us (7%)
  other arithmetic  0.85 us (1%)
  between operations  0.82 us (1%)
    ppermute x6, starting transfers between devices, sent_along(): return lax.ppermute(value, 'space', pairs)  33.7 us
    all_to_all x2, starting transfers between devices, exchanged(): return lax.all_to_all(x, axis, 0, 0, tiled=True, axis_index_groups=members)  17.1 us
    all_to_all x1, blocking collectives, exchanged(): return lax.all_to_all(x, axis, 0, 0, tiled=True, axis_index_groups=members)  11.3 us
    all_to_all x2, waiting for transfers between devices, exchanged(): return lax.all_to_all(x, axis, 0, 0, tiled=True, axis_index_groups=members)  8.48 us
    pallas_call x5, Pallas kernels, call(): pl.pallas_call(body, out_shape=tuple((jax.ShapeDtypeStruct(shape, dtype)...  5.54 us
    ppermute x6, waiting for transfers between devices, sent_along(): return lax.ppermute(value, 'space', pairs)  1.89 us
  transfers between devices with their start and end apart: 8, of which 2 were waited for; matrix products, arithmetic and copies ran while one was open for 0% of the time, Pallas kernels for 5%

commit v1 on v0

--- a/solution.py
+++ b/solution.py
@@ -63,10 +63,8 @@
     hids[2 * CIN : 3 * CIN, (YC - 1) * ZC : YC * ZC] = none
 
 
-def own_kernel(
-    act_hbm, own_hbm, w_hbm, grad_ref, tap_ref, sum_ref, up_ref, down_ref, act_ref, own_ref, w_ref, wide, acts, hids, mids, sems
-):
-    pairs = ((own_hbm, own_ref), (act_hbm, act_ref), (w_hbm, w_ref))
+def own_kernel(act_hbm, own_hbm, grad_ref, tap_ref, act_ref, own_ref, wide, acts, hids, sems):
+    pairs = ((own_hbm, own_ref), (act_hbm, act_ref))
     copies = [pltpu.make_async_copy(a, b, sems.at[i]) for i, (a, b) in enumerate(pairs)]
     for copy in copies:
         copy.start()
@@ -74,15 +72,7 @@
     spread(own_ref, wide, grad_ref, 0)
     copies[1].wait()
     stack_hidden(act_ref[...].astype(jnp.float32), acts, hids)
-    copies[2].wait()
-    for v in range(3):
-        for w in range(3):
-            rows, lanes = slice(v * CIN, (v + 1) * CIN), slice(w * COUT, (w + 1) * COUT)
-            down_ref[rows, lanes] = w_ref[3 * v + w]
-            mids[rows, lanes] = w_ref[9 + 3 * v + w]
-            up_ref[rows, lanes] = w_ref[18 + 3 * v + w]
     tap_ref[...] = by_taps(hids, grad_ref)
-    sum_ref[...] = by_cells(mids, grad_ref)
 
 
 def chosen(take, swapped, straight):
@@ -115,15 +105,23 @@
 
 
 def grad_kernel(
-    at_ref, act_ref, low_ref, high_ref, swap_ref, sum_ref, up_ref, down_ref, gin_ref, plane, wide, acts, grads
+    at_ref, act_ref, own_ref, low_ref, high_ref, swap_ref, w_ref, gin_ref, plane, wide, acts, grads, weights
 ):
+    def part(u, moved):
+        for v in range(3):
+            for w in range(3):
+                rows, lanes = slice(v * CIN, (v + 1) * CIN), slice(w * COUT, (w + 1) * COUT)
+                weights[rows, lanes] = w_ref[9 * u + 3 * v + w]
+        return by_cells(weights, moved)
+
     at = at_ref[0, 0]
+    sums = part(1, own_ref)
     plane[...] = chosen(at == 0, swap_ref, low_ref)
     spread(plane, wide, grads, 0)
-    sums = by_cells(up_ref, grads) + sum_ref[...]
+    sums = sums + part(2, grads)
     plane[...] = chosen(at == ZL - 1, swap_ref, high_ref)
     spread(plane, wide, grads, 0)
-    sums = sums + by_cells(down_ref, grads)
+    sums = sums + part(0, grads)
     for y in range(YC):
         total = sums[CIN : 2 * CIN, y * ZC : (y + 1) * ZC]
         if y + 1 < YC:
@@ -215,13 +213,12 @@
     plane = ((COUT * YC, ZC), f32)
     small = ((CIN * YC, ZC), f32)
     stacked, moved, third = ((3 * CIN, CELLS), bf16), ((3 * COUT, CELLS), bf16), ((3 * CIN, 3 * COUT), bf16)
-    grads, taps, sums, up, down = call(
+    grads, taps = call(
         own_kernel,
-        [moved, ((3 * CIN, 3 * COUT), f32), ((3 * CIN, CELLS), f32), third, third],
-        [(act.shape, bf16), (own.shape, bf16), (weight.shape, bf16), plane, small, stacked, third]
-        + [pltpu.SemaphoreType.DMA((3,))],
+        [moved, ((3 * CIN, 3 * COUT), f32)],
+        [(act.shape, bf16), (own.shape, bf16), plane, small, stacked, pltpu.SemaphoreType.DMA((2,))],
         1_000_000_000,
-        *[pltpu.with_memory_space_constraint(x, pltpu.HBM) for x in (act, own, weight)],
+        *[pltpu.with_memory_space_constraint(x, pltpu.HBM) for x in (act, own)],
         inputs=pltpu.HBM,
     )
     start = (lax.axis_index("batch") & 3) * 32
@@ -241,13 +238,13 @@
     swap_grad = sent_along(own, turns)
     got = exchanged(sent.astype(f16), "batch", along_y).astype(f32)
     (sent,) = call(after_y_kernel, [((ZS, PART, COUT), f32)], [], 1_000_000, got)
-    sums, _ = lax.optimization_barrier((sums, sent))
+    grads, _ = lax.optimization_barrier((grads, sent))
     (grad_in,) = call(
         grad_kernel,
         [((CIN, YC, ZC), bf16)],
-        [((COUT, YC, ZC), f32), plane, small, moved],
+        [((COUT, YC, ZC), f32), plane, small, moved, third],
         2_000_000_000,
-        at, act, low, high, swap_grad, sums, up, down,
+        at, act, grads, low, high, swap_grad, weight,
     )
     got = exchanged(sent, ("space", "batch"), along_z)
     total = jnp.sum(got, axis=0).reshape(-1)

time: 80.7 us -> 80.7 us (level)
  no operation moved by 1% of the time
where the time goes in v1:
time: 80.7 us; the launch traced here: 80.3 us
  starting transfers between devices  50.8 us (63%)
  blocking collectives  11.3 us (14%)
  waiting for transfers between devices  10.5 us (13%)
  Pallas kernels  5.44 us (7%)
  other arithmetic  0.85 us (1%)
  between operations  0.84 us (1%)
    ppermute x6, starting transfers between devices, sent_along(): return lax.ppermute(value, 'space', pairs)  33.7 us
    all_to_all x2, starting transfers between devices, exchanged(): return lax.all_to_all(x, axis, 0, 0, tiled=True, axis_index_groups=members)  17.1 us
    all_to_all x1, blocking collectives, exchanged(): return lax.all_to_all(x, axis, 0, 0, tiled=True, axis_index_groups=members)  11.3 us
    all_to_all x2, waiting for transfers between devices, exchanged(): return lax.all_to_all(x, axis, 0, 0, tiled=True, axis_index_groups=members)  8.22 us
    pallas_call x5, Pallas kernels, call(): pl.pallas_call(body, out_shape=tuple((jax.ShapeDtypeStruct(shape, dtype)...  5.44 us
    ppermute x6, waiting for transfers between devices, sent_along(): return lax.ppermute(value, 'space', pairs)  2.23 us
  transfers between devices with their start and end apart: 8, of which 2 were waited for; matrix products, arithmetic and copies ran while one was open for 0% of the time, Pallas kernels for 5%

profile of v1, /device:TPU:10, one launch (start us, length us, event | category | flops | bytes accessed | tf_op | source)
XLA Modules:
  0.0 80.3 jit_solution(5295318398030881609)
XLA Ops:
  0.6 4.3 %collective-permute-start = (bf16[64,8,128]{2,1,0:T(8,128)(2,1)}, bf16[64,8,128]{2,1,0:T(8,128)(2,1)S(1)}, u32[]{:S(2)}, u32[]{:S(2)}) collective-permute-start(bf16[64,8,128]{2,1,0:T(8,128)(2,1)} %bitcast.7), channel_id=1, source_target_pairs={{0,32},{32,64},{64,96},{96,128},{128,160},{192,224},{224,256},{256... | collective-permute-start | bytes 393224 | tf_op jit(solution)/shard_map/ppermute | solution.py:193
  4.9 1.3 %collective-permute-start.1 = (bf16[64,8,128]{2,1,0:T(8,128)(2,1)}, bf16[64,8,128]{2,1,0:T(8,128)(2,1)S(1)}, u32[]{:S(2)}, u32[]{:S(2)}) collective-permute-start(bf16[64,8,128]{2,1,0:T(8,128)(2,1)} %bitcast.8), channel_id=1, source_target_pairs={{32,0},{64,32},{96,64},{128,96},{160,128},{224,192},{256,224},{288... | collective-permute-start | bytes 393224 | tf_op jit(solution)/shard_map/ppermute | solution.py:193
  6.2 13.0 %collective-permute-start.2 = (bf16[64,8,128]{2,1,0:T(8,128)(2,1)}, bf16[64,8,128]{2,1,0:T(8,128)(2,1)S(1)}, u32[]{:S(2)}, u32[]{:S(2)}) collective-permute-start(bf16[64,8,128]{2,1,0:T(8,128)(2,1)} %bitcast.9), channel_id=1, source_target_pairs={{160,192},{352,384},{544,576},{192,160},{384,352},{576,544},{161,1... | collective-permute-start | bytes 393224 | tf_op jit(solution)/shard_map/ppermute | solution.py:193
  19.2 1.7 %shard_map.50 = (bf16[384,1024]{1,0:T(8,128)(2,1)S(1)}, f32[192,384]{1,0:T(8,128)S(1)}) custom-call(bf16[64,8,128]{2,1,0:T(8,128)(2,1)} %bitcast.10, bf16[128,8,128]{2,1,0:T(8,128)(2,1)} %bitcast.13), custom_call_target="tpu_custom_call" | custom-call | flops 1000000000 | bytes 2000000 | tf_op jit(solution)/shard_map/pallas_call | solution.py:161
  21.0 0.0 collective-permute-done.low_ref
  21.0 0.0 collective-permute-done.1.high_ref
  21.0 2.2 %collective-permute-done.2.swap_ref = bf16[64,8,128]{2,1,0:T(8,128)(2,1)S(1)} collective-permute-done((bf16[64,8,128]{2,1,0:T(8,128)(2,1)}, bf16[64,8,128]{2,1,0:T(8,128)(2,1)S(1)}, u32[]{:S(2)}, u32[]{:S(2)}) %collective-permute-start.2) | collective-permute-done | bytes 131104 | tf_op jit(solution)/shard_map/ppermute | solution.py:193
  23.2 1.1 %shard_map.51 = f32[4,440,128]{2,1,0:T(8,128)S(1)} custom-call(s32[1,1]{1,0:T(1,128)} %bitcast.at_ref, bf16[64,8,128]{2,1,0:T(8,128)(2,1)S(1)} %collective-permute-done.low_ref, bf16[64,8,128]{2,1,0:T(8,128)(2,1)S(1)} %collective-permute-done.1.high_ref, bf16[64,8,128]{2,1,0:T(8,128)(2,1)S(1)} %collective-permute-done.2.swap_ref, ...), custom_call_target="tpu_custom_call" | custom-call | flops 1000000000 | bytes 2000000 | tf_op jit(solution)/shard_map/pallas_call | solution.py:161
  24.3 0.1 convert_element_type.12
  24.4 11.3 %all_to_all.15 = f16[4,440,128]{2,1,0:T(8,128)(2,1)S(1)} all-to-all(f16[4,440,128]{2,1,0:T(8,128)(2,1)S(1)} %convert_element_type.12), channel_id=1, replica_groups={{0,192,384,576},{32,224,416,608},{64,256,448,640},{96,288,480,672},{128..., dimensions={0} | all-to-all | bytes 901120 | tf_op jit(solution)/shard_map/all_to_all | solution.py:189
  35.6 0.1 convert_element_type.13.got_ref
  35.7 0.1 shard_map.52
  35.8 0.7 convert_element_type.14
  36.5 0.0 copy-start.2
  36.5 7.7 %all-to-all-start.1 = ((f16[16,40,128]{2,1,0:T(8,128)(2,1)}), f16[16,40,128]{2,1,0:T(8,128)(2,1)S(1)}, u32[]{:S(2)}, u32[]{:S(2)}) async-start(f16[16,40,128]{2,1,0:T(8,128)(2,1)} %convert_element_type.14), calls=%async_computation.1 | async-start | bytes 327680 | tf_op jit(solution)/shard_map/all_to_all | solution.py:189
  44.2 0.0 copy-done.2
  44.2 1.3 %collective-permute-start.3 = (bf16[128,8,128]{2,1,0:T(8,128)(2,1)S(1)}, bf16[128,8,128]{2,1,0:T(8,128)(2,1)S(1)}, u32[]{:S(2)}, u32[]{:S(2)}) collective-permute-start(bf16[128,8,128]{2,1,0:T(8,128)(2,1)S(1)} %bitcast.14), channel_id=1, source_target_pairs={{0,32},{32,64},{64,96},{96,128},{128,160},{192,224},{224,256},{256... | collective-permute-start | bytes 786440 | tf_op jit(solution)/shard_map/ppermute | solution.py:193
  45.5 1.3 %collective-permute-start.4 = (bf16[128,8,128]{2,1,0:T(8,128)(2,1)S(1)}, bf16[128,8,128]{2,1,0:T(8,128)(2,1)S(1)}, u32[]{:S(2)}, u32[]{:S(2)}) collective-permute-start(bf16[128,8,128]{2,1,0:T(8,128)(2,1)S(1)} %bitcast.15), channel_id=1, source_target_pairs={{32,0},{64,32},{96,64},{128,96},{160,128},{224,192},{256,224},{288... | collective-permute-start | bytes 786440 | tf_op jit(solution)/shard_map/ppermute | solution.py:193
  46.8 12.5 %collective-permute-start.5 = (bf16[128,8,128]{2,1,0:T(8,128)(2,1)S(1)}, bf16[128,8,128]{2,1,0:T(8,128)(2,1)S(1)}, u32[]{:S(2)}, u32[]{:S(2)}) collective-permute-start(bf16[128,8,128]{2,1,0:T(8,128)(2,1)S(1)} %bitcast.16), channel_id=1, source_target_pairs={{160,192},{352,384},{544,576},{192,160},{384,352},{576,544},{161,1... | collective-permute-start | bytes 786440 | tf_op jit(solution)/shard_map/ppermute | solution.py:193
  59.4 0.0 copy-start
  59.4 0.0 all-to-all-done.1
  59.4 0.0 copy-start.1
  59.4 0.7 shard_map.53
  60.1 9.4 %all-to-all-start.2 = ((f32[12,3,128]{2,1,0:T(4,128)}), f32[12,3,128]{2,1,0:T(4,128)S(1)}, u32[]{:S(2)}, u32[]{:S(2)}) async-start(f32[12,3,128]{2,1,0:T(4,128)} %shard_map.53), calls=%async_computation.2 | async-start | bytes 49152 | tf_op jit(solution)/shard_map/all_to_all | solution.py:189
  69.5 0.0 collective-permute-done.3.low_ref
  69.5 0.0 collective-permute-done.4.high_ref
  69.5 0.0 collective-permute-done.5.swap_ref
  69.6 0.0 copy-done
  69.6 0.0 copy-done.1
  69.6 1.8 %shard_map.54 = bf16[64,8,128]{2,1,0:T(8,128)(2,1)} custom-call(s32[1,1]{1,0:T(1,128)} %bitcast.at_ref, bf16[64,8,128]{2,1,0:T(8,128)(2,1)S(1)} %bitcast.11, bf16[384,1024]{1,0:T(8,128)(2,1)S(1)} %get-tuple-element.15.grad_ref.own_ref, bf16[128,8,128]{2,1,0:T(8,128)(2,1)S(1)} %collective-permute-done.3.low_ref, ...), custom_call_target="tpu_custom_call" | custom-call | flops 2000000000 | bytes 2000000 | tf_op jit(solution)/shard_map/pallas_call | solution.py:161
  71.4 8.2 %all-to-all-done.2 = f32[12,3,128]{2,1,0:T(4,128)S(1)} async-done(((f32[12,3,128]{2,1,0:T(4,128)}), f32[12,3,128]{2,1,0:T(4,128)S(1)}, u32[]{:S(2)}, u32[]{:S(2)}) %all-to-all-start.2) | async-done | bytes 18464 | tf_op jit(solution)/shard_map/all_to_all | solution.py:189
  79.7 0.7 dynamic_slice.3
  (2 shorter events, 0.0 us)
Async XLA Ops:
  0.6 20.4 %collective-permute-start = (bf16[64,8,128]{2,1,0:T(8,128)(2,1)}, bf16[64,8,128]{2,1,0:T(8,128)(2,1)S(1)}, u32[]{:S(2)}, u32[]{:S(2)}) collective-permute-start(bf16[64,8,128]{2,1,0:T(8,128)(2,1)} %bitcast.7), channel_id=1, source_target_pairs={{0,32},{32,64},{64,96},{96,128},{128,160},{192,224},{224,256},{256... | collective-permute-start | bytes 393224 | tf_op jit(solution)/shard_map/ppermute | solution.py:193
  4.9 16.1 %collective-permute-start.1 = (bf16[64,8,128]{2,1,0:T(8,128)(2,1)}, bf16[64,8,128]{2,1,0:T(8,128)(2,1)S(1)}, u32[]{:S(2)}, u32[]{:S(2)}) collective-permute-start(bf16[64,8,128]{2,1,0:T(8,128)(2,1)} %bitcast.8), channel_id=1, source_target_pairs={{32,0},{64,32},{96,64},{128,96},{160,128},{224,192},{256,224},{288... | collective-permute-start | bytes 393224 | tf_op jit(solution)/shard_map/ppermute | solution.py:193
  6.2 17.0 %collective-permute-start.2 = (bf16[64,8,128]{2,1,0:T(8,128)(2,1)}, bf16[64,8,128]{2,1,0:T(8,128)(2,1)S(1)}, u32[]{:S(2)}, u32[]{:S(2)}) collective-permute-start(bf16[64,8,128]{2,1,0:T(8,128)(2,1)} %bitcast.9), channel_id=1, source_target_pairs={{160,192},{352,384},{544,576},{192,160},{384,352},{576,544},{161,1... | collective-permute-start | bytes 393224 | tf_op jit(solution)/shard_map/ppermute | solution.py:193
  36.5 7.7 %copy-start.2 = (bf16[1,128,1,8,128]{4,3,2,1,0:T(8,128)(2,1)S(1)}, bf16[1,128,1,8,128]{4,3,2,1,0:T(8,128)(2,1)}, u32[]{:S(2)}) copy-start(bf16[1,128,1,8,128]{4,3,2,1,0:T(8,128)(2,1)} %param.4) | copy-start | bytes 786436
  36.5 22.9 %all-to-all-start.1 = ((f16[16,40,128]{2,1,0:T(8,128)(2,1)}), f16[16,40,128]{2,1,0:T(8,128)(2,1)S(1)}, u32[]{:S(2)}, u32[]{:S(2)}) async-start(f16[16,40,128]{2,1,0:T(8,128)(2,1)} %convert_element_type.14), calls=%async_computation.1 | async-start | bytes 327680 | tf_op jit(solution)/shard_map/all_to_all | solution.py:189
  44.2 25.3 %collective-permute-start.3 = (bf16[128,8,128]{2,1,0:T(8,128)(2,1)S(1)}, bf16[128,8,128]{2,1,0:T(8,128)(2,1)S(1)}, u32[]{:S(2)}, u32[]{:S(2)}) collective-permute-start(bf16[128,8,128]{2,1,0:T(8,128)(2,1)S(1)} %bitcast.14), channel_id=1, source_target_pairs={{0,32},{32,64},{64,96},{96,128},{128,160},{192,224},{224,256},{256... | collective-permute-start | bytes 786440 | tf_op jit(solution)/shard_map/ppermute | solution.py:193
  45.5 24.0 %collective-permute-start.4 = (bf16[128,8,128]{2,1,0:T(8,128)(2,1)S(1)}, bf16[128,8,128]{2,1,0:T(8,128)(2,1)S(1)}, u32[]{:S(2)}, u32[]{:S(2)}) collective-permute-start(bf16[128,8,128]{2,1,0:T(8,128)(2,1)S(1)} %bitcast.15), channel_id=1, source_target_pairs={{32,0},{64,32},{96,64},{128,96},{160,128},{224,192},{256,224},{288... | collective-permute-start | bytes 786440 | tf_op jit(solution)/shard_map/ppermute | solution.py:193
  46.8 22.7 %collective-permute-start.5 = (bf16[128,8,128]{2,1,0:T(8,128)(2,1)S(1)}, bf16[128,8,128]{2,1,0:T(8,128)(2,1)S(1)}, u32[]{:S(2)}, u32[]{:S(2)}) collective-permute-start(bf16[128,8,128]{2,1,0:T(8,128)(2,1)S(1)} %bitcast.16), channel_id=1, source_target_pairs={{160,192},{352,384},{544,576},{192,160},{384,352},{576,544},{161,1... | collective-permute-start | bytes 786440 | tf_op jit(solution)/shard_map/ppermute | solution.py:193
  59.4 10.2 %copy-start = (bf16[27,64,128]{2,1,0:T(8,128)(2,1)S(1)}, bf16[27,64,128]{2,1,0:T(8,128)(2,1)}, u32[]{:S(2)}) copy-start(bf16[27,64,128]{2,1,0:T(8,128)(2,1)} %w_ref.1) | copy-start | bytes 1327108
  59.4 10.2 %copy-start.1 = (bf16[1,64,1,8,128]{4,3,2,1,0:T(8,128)(2,1)S(1)}, bf16[1,64,1,8,128]{4,3,2,1,0:T(8,128)(2,1)}, u32[]{:S(2)}) copy-start(bf16[1,64,1,8,128]{4,3,2,1,0:T(8,128)(2,1)} %param.3) | copy-start | bytes 393220
  60.1 19.6 %all-to-all-start.2 = ((f32[12,3,128]{2,1,0:T(4,128)}), f32[12,3,128]{2,1,0:T(4,128)S(1)}, u32[]{:S(2)}, u32[]{:S(2)}) async-start(f32[12,3,128]{2,1,0:T(4,128)} %shard_map.53), calls=%async_computation.2 | async-start | bytes 49152 | tf_op jit(solution)/shard_map/all_to_all | solution.py:189

commit v2 on v1

--- a/solution.py
+++ b/solution.py
@@ -63,7 +63,7 @@
     hids[2 * CIN : 3 * CIN, (YC - 1) * ZC : YC * ZC] = none
 
 
-def own_kernel(act_hbm, own_hbm, grad_ref, tap_ref, act_ref, own_ref, wide, acts, hids, sems):
+def own_kernel(act_hbm, own_hbm, grad_ref, tap_ref, kept_ref, act_ref, own_ref, wide, acts, hids, sems):
     pairs = ((own_hbm, own_ref), (act_hbm, act_ref))
     copies = [pltpu.make_async_copy(a, b, sems.at[i]) for i, (a, b) in enumerate(pairs)]
     for copy in copies:
@@ -73,6 +73,11 @@
     copies[1].wait()
     stack_hidden(act_ref[...].astype(jnp.float32), acts, hids)
     tap_ref[...] = by_taps(hids, grad_ref)
+    kept_ref[...] = own_ref[...]
+
+
+def keep_kernel(own_ref, kept_ref):
+    kept_ref[...] = own_ref[...]
 
 
 def chosen(take, swapped, straight):
@@ -213,9 +218,9 @@
     plane = ((COUT * YC, ZC), f32)
     small = ((CIN * YC, ZC), f32)
     stacked, moved, third = ((3 * CIN, CELLS), bf16), ((3 * COUT, CELLS), bf16), ((3 * CIN, 3 * COUT), bf16)
-    grads, taps = call(
+    grads, taps, kept = call(
         own_kernel,
-        [moved, ((3 * CIN, 3 * COUT), f32)],
+        [moved, ((3 * CIN, 3 * COUT), f32), (own.shape, bf16)],
         [(act.shape, bf16), (own.shape, bf16), plane, small, stacked, pltpu.SemaphoreType.DMA((2,))],
         1_000_000_000,
         *[pltpu.with_memory_space_constraint(x, pltpu.HBM) for x in (act, own)],
@@ -231,11 +236,14 @@
         1_000_000_000,
         at, low_act, high_act, swap_act, grads, taps,
     )
-    got = exchanged(sent.astype(f16), "space", along_x).astype(f32)
-    (sent,) = call(after_x_kernel, [((YCS, PART * ZS + YMARKS, COUT), f32)], [((XROWS, COUT), f32)], 1_000_000, got)
+    got = exchanged(sent.astype(f16), "space", along_x)
+    (kept,) = call(keep_kernel, [(own.shape, bf16)], [], 1_000_000, kept)
+    swap_grad = sent_along(kept, turns)
+    (sent,) = call(
+        after_x_kernel, [((YCS, PART * ZS + YMARKS, COUT), f32)], [((XROWS, COUT), f32)], 1_000_000, got.astype(f32)
+    )
     own, sent = lax.optimization_barrier((own, sent))
     high = sent_along(own, backward)
-    swap_grad = sent_along(own, turns)
     got = exchanged(sent.astype(f16), "batch", along_y).astype(f32)
     (sent,) = call(after_y_kernel, [((ZS, PART, COUT), f32)], [], 1_000_000, got)
     grads, _ = lax.optimization_barrier((grads, sent))

time: 80.7 us -> 78.7 us (0.975)
  starting transfers between devices: 50.8 us -> 48.7 us
    ppermute x6, starting transfers between devices: 33.7 us -> 30.4 us  [sent_along(): return lax.ppermute(value, 'space', pairs)]
    all_to_all x2, starting transfers between devices: 17.1 us -> 18.3 us  [exchanged(): return lax.all_to_all(x, axis, 0, 0, tiled=True, axis_index_groups=members)]
    pallas_call x5 -> x6, Pallas kernels: 5.44 us -> 5.48 us  [call(): pl.pallas_call(body, out_shape=tuple((jax.ShapeDtypeStruct(shape, dtype)...]
where the time goes in v2:
time: 78.7 us; the launch traced here: 78.3 us
  starting transfers between devices  48.7 us (62%)
  blocking collectives  11.3 us (14%)
  waiting for transfers between devices  10.4 us (13%)
  Pallas kernels  5.48 us (7%)
  other arithmetic  0.85 us (1%)
  between operations  0.84 us (1%)
    ppermute x6, starting transfers between devices, sent_along(): return lax.ppermute(value, 'space', pairs)  30.4 us
    all_to_all x2, starting transfers between devices, exchanged(): return lax.all_to_all(x, axis, 0, 0, tiled=True, axis_index_groups=members)  18.3 us
    all_to_all x1, blocking collectives, exchanged(): return lax.all_to_all(x, axis, 0, 0, tiled=True, axis_index_groups=members)  11.3 us
    all_to_all x2, waiting for transfers between devices, exchanged(): return lax.all_to_all(x, axis, 0, 0, tiled=True, axis_index_groups=members)  8.22 us
    pallas_call x6, Pallas kernels, call(): pl.pallas_call(body, out_shape=tuple((jax.ShapeDtypeStruct(shape, dtype)...  5.48 us
    ppermute x6, waiting for transfers between devices, sent_along(): return lax.ppermute(value, 'space', pairs)  2.21 us
  transfers between devices with their start and end apart: 8, of which 2 were waited for; matrix products, arithmetic and copies ran while one was open for 0% of the time, Pallas kernels for 5%

profile of v2, /device:TPU:10, one launch (start us, length us, event | category | flops | bytes accessed | tf_op | source)
XLA Modules:
  0.0 78.3 jit_solution(12665477190227736916)
XLA Ops:
  0.6 4.3 %collective-permute-start = (bf16[64,8,128]{2,1,0:T(8,128)(2,1)}, bf16[64,8,128]{2,1,0:T(8,128)(2,1)S(1)}, u32[]{:S(2)}, u32[]{:S(2)}) collective-permute-start(bf16[64,8,128]{2,1,0:T(8,128)(2,1)} %bitcast.7), channel_id=1, source_target_pairs={{0,32},{32,64},{64,96},{96,128},{128,160},{192,224},{224,256},{256... | collective-permute-start | bytes 393224 | tf_op jit(solution)/shard_map/ppermute | solution.py:198
  4.9 1.3 %collective-permute-start.1 = (bf16[64,8,128]{2,1,0:T(8,128)(2,1)}, bf16[64,8,128]{2,1,0:T(8,128)(2,1)S(1)}, u32[]{:S(2)}, u32[]{:S(2)}) collective-permute-start(bf16[64,8,128]{2,1,0:T(8,128)(2,1)} %bitcast.8), channel_id=1, source_target_pairs={{32,0},{64,32},{96,64},{128,96},{160,128},{224,192},{256,224},{288... | collective-permute-start | bytes 393224 | tf_op jit(solution)/shard_map/ppermute | solution.py:198
  6.2 13.0 %collective-permute-start.2 = (bf16[64,8,128]{2,1,0:T(8,128)(2,1)}, bf16[64,8,128]{2,1,0:T(8,128)(2,1)S(1)}, u32[]{:S(2)}, u32[]{:S(2)}) collective-permute-start(bf16[64,8,128]{2,1,0:T(8,128)(2,1)} %bitcast.9), channel_id=1, source_target_pairs={{160,192},{352,384},{544,576},{192,160},{384,352},{576,544},{161,1... | collective-permute-start | bytes 393224 | tf_op jit(solution)/shard_map/ppermute | solution.py:198
  19.2 1.8 %shard_map.50 = (bf16[384,1024]{1,0:T(8,128)(2,1)S(1)}, f32[192,384]{1,0:T(8,128)S(1)}, bf16[128,8,128]{2,1,0:T(8,128)(2,1)S(1)}) custom-call(bf16[64,8,128]{2,1,0:T(8,128)(2,1)} %bitcast.10, bf16[128,8,128]{2,1,0:T(8,128)(2,1)} %bitcast.13), custom_call_target="tpu_custom_call" | custom-call | flops 1000000000 | bytes 2000000 | tf_op jit(solution)/shard_map/pallas_call | solution.py:166
  21.0 0.0 collective-permute-done.low_ref
  21.0 0.0 collective-permute-done.1.high_ref
  21.0 2.2 %collective-permute-done.2.swap_ref = bf16[64,8,128]{2,1,0:T(8,128)(2,1)S(1)} collective-permute-done((bf16[64,8,128]{2,1,0:T(8,128)(2,1)}, bf16[64,8,128]{2,1,0:T(8,128)(2,1)S(1)}, u32[]{:S(2)}, u32[]{:S(2)}) %collective-permute-start.2) | collective-permute-done | bytes 131104 | tf_op jit(solution)/shard_map/ppermute | solution.py:198
  23.2 1.1 %shard_map.51 = f32[4,440,128]{2,1,0:T(8,128)S(1)} custom-call(s32[1,1]{1,0:T(1,128)} %bitcast.at_ref, bf16[64,8,128]{2,1,0:T(8,128)(2,1)S(1)} %collective-permute-done.low_ref, bf16[64,8,128]{2,1,0:T(8,128)(2,1)S(1)} %collective-permute-done.1.high_ref, bf16[64,8,128]{2,1,0:T(8,128)(2,1)S(1)} %collective-permute-done.2.swap_ref, ...), custom_call_target="tpu_custom_call" | custom-call | flops 1000000000 | bytes 2000000 | tf_op jit(solution)/shard_map/pallas_call | solution.py:166
  24.3 0.1 convert_element_type.12
  24.4 11.3 %all_to_all.15 = f16[4,440,128]{2,1,0:T(8,128)(2,1)S(1)} all-to-all(f16[4,440,128]{2,1,0:T(8,128)(2,1)S(1)} %convert_element_type.12), channel_id=1, replica_groups={{0,192,384,576},{32,224,416,608},{64,256,448,640},{96,288,480,672},{128..., dimensions={0} | all-to-all | bytes 901120 | tf_op jit(solution)/shard_map/all_to_all | solution.py:194
  35.6 0.1 convert_element_type.13.got_ref
  35.7 0.1 shard_map.52
  35.8 0.7 convert_element_type.14
  36.5 0.0 copy-start.2
  36.5 7.7 %all-to-all-start.1 = ((f16[16,40,128]{2,1,0:T(8,128)(2,1)}), f16[16,40,128]{2,1,0:T(8,128)(2,1)S(1)}, u32[]{:S(2)}, u32[]{:S(2)}) async-start(f16[16,40,128]{2,1,0:T(8,128)(2,1)} %convert_element_type.14), calls=%async_computation.1 | async-start | bytes 327680 | tf_op jit(solution)/shard_map/all_to_all | solution.py:194
  44.2 0.0 copy-done.2
  44.2 1.3 %collective-permute-start.3 = (bf16[128,8,128]{2,1,0:T(8,128)(2,1)S(1)}, bf16[128,8,128]{2,1,0:T(8,128)(2,1)S(1)}, u32[]{:S(2)}, u32[]{:S(2)}) collective-permute-start(bf16[128,8,128]{2,1,0:T(8,128)(2,1)S(1)} %bitcast.14), channel_id=1, source_target_pairs={{0,32},{32,64},{64,96},{96,128},{128,160},{192,224},{224,256},{256... | collective-permute-start | bytes 786440 | tf_op jit(solution)/shard_map/ppermute | solution.py:198
  45.6 9.2 %collective-permute-start.5 = (bf16[128,8,128]{2,1,0:T(8,128)(2,1)S(1)}, bf16[128,8,128]{2,1,0:T(8,128)(2,1)S(1)}, u32[]{:S(2)}, u32[]{:S(2)}) collective-permute-start(bf16[128,8,128]{2,1,0:T(8,128)(2,1)S(1)} %shard_map.54), channel_id=1, source_target_pairs={{160,192},{352,384},{544,576},{192,160},{384,352},{576,544},{161,1... | collective-permute-start | bytes 786440 | tf_op jit(solution)/shard_map/ppermute | solution.py:198
  54.8 1.3 %collective-permute-start.4 = (bf16[128,8,128]{2,1,0:T(8,128)(2,1)S(1)}, bf16[128,8,128]{2,1,0:T(8,128)(2,1)S(1)}, u32[]{:S(2)}, u32[]{:S(2)}) collective-permute-start(bf16[128,8,128]{2,1,0:T(8,128)(2,1)S(1)} %bitcast.15), channel_id=1, source_target_pairs={{32,0},{64,32},{96,64},{128,96},{160,128},{224,192},{256,224},{288... | collective-permute-start | bytes 786440 | tf_op jit(solution)/shard_map/ppermute | solution.py:198
  56.1 0.0 copy-start
  56.1 0.0 all-to-all-done.1
  56.2 0.0 copy-start.1
  56.2 0.7 shard_map.53
  56.8 10.6 %all-to-all-start.2 = ((f32[12,3,128]{2,1,0:T(4,128)}), f32[12,3,128]{2,1,0:T(4,128)S(1)}, u32[]{:S(2)}, u32[]{:S(2)}) async-start(f32[12,3,128]{2,1,0:T(4,128)} %shard_map.53), calls=%async_computation.2 | async-start | bytes 49152 | tf_op jit(solution)/shard_map/all_to_all | solution.py:194
  67.5 0.0 collective-permute-done.5.swap_ref
  67.5 0.0 collective-permute-done.3.low_ref
  67.5 0.0 collective-permute-done.4.high_ref
  67.5 0.0 copy-done
  67.5 0.0 copy-done.1
  67.5 1.8 %shard_map.55 = bf16[64,8,128]{2,1,0:T(8,128)(2,1)} custom-call(s32[1,1]{1,0:T(1,128)} %bitcast.at_ref, bf16[64,8,128]{2,1,0:T(8,128)(2,1)S(1)} %bitcast.11, bf16[384,1024]{1,0:T(8,128)(2,1)S(1)} %get-tuple-element.16.grad_ref.own_ref, bf16[128,8,128]{2,1,0:T(8,128)(2,1)S(1)} %collective-permute-done.3.low_ref, ...), custom_call_target="tpu_custom_call" | custom-call | flops 2000000000 | bytes 2000000 | tf_op jit(solution)/shard_map/pallas_call | solution.py:166
  69.4 8.2 %all-to-all-done.2 = f32[12,3,128]{2,1,0:T(4,128)S(1)} async-done(((f32[12,3,128]{2,1,0:T(4,128)}), f32[12,3,128]{2,1,0:T(4,128)S(1)}, u32[]{:S(2)}, u32[]{:S(2)}) %all-to-all-start.2) | async-done | bytes 18464 | tf_op jit(solution)/shard_map/all_to_all | solution.py:194
  77.6 0.7 dynamic_slice.3
  (3 shorter events, 0.1 us)
Async XLA Ops:
  0.6 20.4 %collective-permute-start = (bf16[64,8,128]{2,1,0:T(8,128)(2,1)}, bf16[64,8,128]{2,1,0:T(8,128)(2,1)S(1)}, u32[]{:S(2)}, u32[]{:S(2)}) collective-permute-start(bf16[64,8,128]{2,1,0:T(8,128)(2,1)} %bitcast.7), channel_id=1, source_target_pairs={{0,32},{32,64},{64,96},{96,128},{128,160},{192,224},{224,256},{256... | collective-permute-start | bytes 393224 | tf_op jit(solution)/shard_map/ppermute | solution.py:198
  4.9 16.1 %collective-permute-start.1 = (bf16[64,8,128]{2,1,0:T(8,128)(2,1)}, bf16[64,8,128]{2,1,0:T(8,128)(2,1)S(1)}, u32[]{:S(2)}, u32[]{:S(2)}) collective-permute-start(bf16[64,8,128]{2,1,0:T(8,128)(2,1)} %bitcast.8), channel_id=1, source_target_pairs={{32,0},{64,32},{96,64},{128,96},{160,128},{224,192},{256,224},{288... | collective-permute-start | bytes 393224 | tf_op jit(solution)/shard_map/ppermute | solution.py:198
  6.2 17.0 %collective-permute-start.2 = (bf16[64,8,128]{2,1,0:T(8,128)(2,1)}, bf16[64,8,128]{2,1,0:T(8,128)(2,1)S(1)}, u32[]{:S(2)}, u32[]{:S(2)}) collective-permute-start(bf16[64,8,128]{2,1,0:T(8,128)(2,1)} %bitcast.9), channel_id=1, source_target_pairs={{160,192},{352,384},{544,576},{192,160},{384,352},{576,544},{161,1... | collective-permute-start | bytes 393224 | tf_op jit(solution)/shard_map/ppermute | solution.py:198
  36.5 7.7 %copy-start.2 = (bf16[1,128,1,8,128]{4,3,2,1,0:T(8,128)(2,1)S(1)}, bf16[1,128,1,8,128]{4,3,2,1,0:T(8,128)(2,1)}, u32[]{:S(2)}) copy-start(bf16[1,128,1,8,128]{4,3,2,1,0:T(8,128)(2,1)} %param.4) | copy-start | bytes 786436
  36.5 19.6 %all-to-all-start.1 = ((f16[16,40,128]{2,1,0:T(8,128)(2,1)}), f16[16,40,128]{2,1,0:T(8,128)(2,1)S(1)}, u32[]{:S(2)}, u32[]{:S(2)}) async-start(f16[16,40,128]{2,1,0:T(8,128)(2,1)} %convert_element_type.14), calls=%async_computation.1 | async-start | bytes 327680 | tf_op jit(solution)/shard_map/all_to_all | solution.py:194
  44.2 23.3 %collective-permute-start.3 = (bf16[128,8,128]{2,1,0:T(8,128)(2,1)S(1)}, bf16[128,8,128]{2,1,0:T(8,128)(2,1)S(1)}, u32[]{:S(2)}, u32[]{:S(2)}) collective-permute-start(bf16[128,8,128]{2,1,0:T(8,128)(2,1)S(1)} %bitcast.14), channel_id=1, source_target_pairs={{0,32},{32,64},{64,96},{96,128},{128,160},{192,224},{224,256},{256... | collective-permute-start | bytes 786440 | tf_op jit(solution)/shard_map/ppermute | solution.py:198
  45.6 21.9 %collective-permute-start.5 = (bf16[128,8,128]{2,1,0:T(8,128)(2,1)S(1)}, bf16[128,8,128]{2,1,0:T(8,128)(2,1)S(1)}, u32[]{:S(2)}, u32[]{:S(2)}) collective-permute-start(bf16[128,8,128]{2,1,0:T(8,128)(2,1)S(1)} %shard_map.54), channel_id=1, source_target_pairs={{160,192},{352,384},{544,576},{192,160},{384,352},{576,544},{161,1... | collective-permute-start | bytes 786440 | tf_op jit(solution)/shard_map/ppermute | solution.py:198
  54.8 12.7 %collective-permute-start.4 = (bf16[128,8,128]{2,1,0:T(8,128)(2,1)S(1)}, bf16[128,8,128]{2,1,0:T(8,128)(2,1)S(1)}, u32[]{:S(2)}, u32[]{:S(2)}) collective-permute-start(bf16[128,8,128]{2,1,0:T(8,128)(2,1)S(1)} %bitcast.15), channel_id=1, source_target_pairs={{32,0},{64,32},{96,64},{128,96},{160,128},{224,192},{256,224},{288... | collective-permute-start | bytes 786440 | tf_op jit(solution)/shard_map/ppermute | solution.py:198
  56.1 11.4 %copy-start = (bf16[27,64,128]{2,1,0:T(8,128)(2,1)S(1)}, bf16[27,64,128]{2,1,0:T(8,128)(2,1)}, u32[]{:S(2)}) copy-start(bf16[27,64,128]{2,1,0:T(8,128)(2,1)} %w_ref.1) | copy-start | bytes 1327108
  56.2 11.3 %copy-start.1 = (bf16[1,64,1,8,128]{4,3,2,1,0:T(8,128)(2,1)S(1)}, bf16[1,64,1,8,128]{4,3,2,1,0:T(8,128)(2,1)}, u32[]{:S(2)}) copy-start(bf16[1,64,1,8,128]{4,3,2,1,0:T(8,128)(2,1)} %param.3) | copy-start | bytes 393220
  56.8 20.7 %all-to-all-start.2 = ((f32[12,3,128]{2,1,0:T(4,128)}), f32[12,3,128]{2,1,0:T(4,128)S(1)}, u32[]{:S(2)}, u32[]{:S(2)}) async-start(f32[12,3,128]{2,1,0:T(4,128)} %shard_map.53), calls=%async_computation.2 | async-start | bytes 49152 | tf_op jit(solution)/shard_map/all_to_all | solution.py:194
